TPU v7x, 32 devices: a whole 2x2x4 slice. The times are simulated.
32 devices in a mesh: gx: 4 (over y, x), gy: 2 (over core), ha: 4 (over z).
Axes of the slice: x: 2, y: 2, z: 4, core: 2. Of those that a mesh axis runs over, the one named last changes fastest.
Arguments:
- level_set: float32 [32, 32, 40, 128], P('gx', 'gy', 'ha'), may hold values from -4 to 4
- wind_field: float32 [2, 32, 32], P(None, 'gx', 'gy'), may hold values from -3 to 3
Outputs:
- increment: float32 [32, 32, 40, 128], P('gx', 'gy', 'ha')
All inputs are finite; a program needn't handle non-finite values.
Results may differ from a plain program's by a relative error of at most 0.000073.
Values sent between devices are 32-bit elements; how exact they have to be, the bound alone decides.
A program may use at most 128 MiB of HBM per device.

v0:
```python
import math

import jax
import jax.numpy as jnp
from jax import lax
from jax.sharding import PartitionSpec as P

CELL_SIZE = 0.05
SPEED_LOW = 0.1
SPEED_SPAN = 0.4
TURN_MAX = 1.0
ACCEL_MAX = 0.05
CFL_NUMBER = 0.5
WENO_EPS = 1e-06


def with_halo(cells, sides, width, closed):
    for axis, dim in sides:
        count = lax.axis_size(axis)
        ends = count if closed else count - 1
        head = lax.slice_in_dim(cells, 0, width, axis=dim)
        tail = lax.slice_in_dim(cells, cells.shape[dim] - width, cells.shape[dim], axis=dim)
        cells = jnp.concatenate(
            [
                lax.ppermute(tail, axis, [(i, (i + 1) % count) for i in range(ends)]),
                cells,
                lax.ppermute(head, axis, [((i + 1) % count, i) for i in range(ends)]),
            ],
            axis=dim,
        )
    return cells


def ghost_rows(values, along, at_low):
    length = values.shape[along]
    if at_low:
        edge_row = lax.slice_in_dim(values, 0, 1, axis=along)
        next_row = lax.slice_in_dim(values, 1, 2, axis=along)
        reaches = (3.0, 2.0, 1.0)
    else:
        edge_row = lax.slice_in_dim(values, length - 1, length, axis=along)
        next_row = lax.slice_in_dim(values, length - 2, length - 1, axis=along)
        reaches = (1.0, 2.0, 3.0)
    slope_edge = edge_row - next_row
    return jnp.concatenate([edge_row + distance * slope_edge for distance in reaches], axis=along)


def fix_edges(extended, along, at_start, at_end, length):
    interior = lax.slice_in_dim(extended, 3, 3 + length, axis=along)
    below_rows = jnp.where(
        at_start, ghost_rows(interior, along, True), lax.slice_in_dim(extended, 0, 3, axis=along)
    )
    above_rows = jnp.where(
        at_end,
        ghost_rows(interior, along, False),
        lax.slice_in_dim(extended, 3 + length, 6 + length, axis=along),
    )
    return jnp.concatenate([below_rows, interior, above_rows], axis=along)


def speed_shifts(values):
    length = values.shape[3]
    below_rows = ghost_rows(values, 3, True)
    above_rows = ghost_rows(values, 3, False)
    shifted = []
    for displace in range(-3, 4):
        pieces = []
        if displace < 0:
            pieces.append(lax.slice_in_dim(below_rows, 3 + displace, 3, axis=3))
        pieces.append(lax.slice_in_dim(values, max(displace, 0), length + min(displace, 0), axis=3))
        if displace > 0:
            pieces.append(lax.slice_in_dim(above_rows, 0, displace, axis=3))
        shifted.append(jnp.concatenate(pieces, axis=3) if len(pieces) > 1 else pieces[0])
    return shifted


def weno_side(left_far, left_near, middle, right_near, right_far):
    guess_one = left_far * (1.0 / 3.0) - left_near * (7.0 / 6.0) + middle * (11.0 / 6.0)
    guess_two = -left_near * (1.0 / 6.0) + middle * (5.0 / 6.0) + right_near * (1.0 / 3.0)
    guess_three = middle * (1.0 / 3.0) + right_near * (5.0 / 6.0) - right_far * (1.0 / 6.0)
    smooth_one = 13.0 / 12.0 * jnp.square(left_far - 2.0 * left_near + middle) + 0.25 * jnp.square(
        left_far - 4.0 * left_near + 3.0 * middle
    )
    smooth_two = 13.0 / 12.0 * jnp.square(
        left_near - 2.0 * middle + right_near
    ) + 0.25 * jnp.square(left_near - right_near)
    smooth_three = 13.0 / 12.0 * jnp.square(
        middle - 2.0 * right_near + right_far
    ) + 0.25 * jnp.square(3.0 * middle - 4.0 * right_near + right_far)
    weight_one = 0.1 / jnp.square(smooth_one + WENO_EPS)
    weight_two = 0.6 / jnp.square(smooth_two + WENO_EPS)
    weight_three = 0.3 / jnp.square(smooth_three + WENO_EPS)
    return (weight_one * guess_one + weight_two * guess_two + weight_three * guess_three) / (
        weight_one + weight_two + weight_three
    )


def weno_pair(shifted, spacing):
    slopes = [(shifted[position + 1] - shifted[position]) / spacing for position in range(6)]
    left_slope = weno_side(slopes[0], slopes[1], slopes[2], slopes[3], slopes[4])
    right_slope = weno_side(slopes[5], slopes[4], slopes[3], slopes[2], slopes[1])
    return (left_slope, right_slope)


def cell_rates(cos_head, sin_head, speeds, wind_x, wind_y, d_theta, d_speed):
    along_x = speeds[None, None, None, :] * cos_head[None, None, :, None] + wind_x[:, :, None, None]
    along_y = speeds[None, None, None, :] * sin_head[None, None, :, None] + wind_y[:, :, None, None]
    return (
        jnp.abs(along_x) / CELL_SIZE
        + jnp.abs(along_y) / CELL_SIZE
        + TURN_MAX / d_theta
        + ACCEL_MAX / d_speed
    )


def hamilton(x_pair, y_pair, head_pair, speed_pair, cos_head, sin_head, speeds, wind_x, wind_y):
    flow_x = speeds[None, None, None, :] * cos_head[None, None, :, None] + wind_x[:, :, None, None]
    flow_y = speeds[None, None, None, :] * sin_head[None, None, :, None] + wind_y[:, :, None, None]
    mean_x = 0.5 * (x_pair[0] + x_pair[1])
    mean_y = 0.5 * (y_pair[0] + y_pair[1])
    mean_head = 0.5 * (head_pair[0] + head_pair[1])
    mean_speed = 0.5 * (speed_pair[0] + speed_pair[1])
    value = -(
        flow_x * mean_x
        + flow_y * mean_y
        + TURN_MAX * jnp.abs(mean_head)
        + ACCEL_MAX * jnp.abs(mean_speed)
    )
    damping = 0.5 * (
        jnp.abs(flow_x) * (x_pair[1] - x_pair[0])
        + jnp.abs(flow_y) * (y_pair[1] - y_pair[0])
        + TURN_MAX * (head_pair[1] - head_pair[0])
        + ACCEL_MAX * (speed_pair[1] - speed_pair[0])
    )
    return -jnp.maximum(value - damping, 0.0)


def body(level_set, wind_field):
    cells_x, cells_y, cells_h, cells_v = level_set.shape
    n_head = cells_h * lax.axis_size("ha")
    head_base = lax.axis_index("ha") * cells_h
    start_x = lax.axis_index("gx") == 0
    end_x = lax.axis_index("gx") == lax.axis_size("gx") - 1
    start_y = lax.axis_index("gy") == 0
    end_y = lax.axis_index("gy") == lax.axis_size("gy") - 1
    wind_x = wind_field[0]
    wind_y = wind_field[1]
    d_theta = 2.0 * math.pi / n_head
    d_speed = SPEED_SPAN / cells_v
    speeds = (
        SPEED_LOW
        + SPEED_SPAN * (jnp.arange(cells_v, dtype=jnp.int32).astype(jnp.float32) + 0.5) / cells_v
    )

    def headings(offset, height):
        slots = (head_base - offset + jnp.arange(height, dtype=jnp.int32) + n_head) % n_head
        angles = slots.astype(jnp.float32) * d_theta
        return (jnp.cos(angles), jnp.sin(angles))

    every_angle = jnp.arange(n_head, dtype=jnp.int32).astype(jnp.float32) * d_theta
    end_speeds = jnp.stack([speeds[0], speeds[cells_v - 1]])
    local_top = jnp.max(
        cell_rates(
            jnp.cos(every_angle), jnp.sin(every_angle), end_speeds, wind_x, wind_y, d_theta, d_speed
        )
    )
    top_rate = lax.pmax(local_top, ("gx", "gy"))
    time_step = CFL_NUMBER / top_rate

    def slope_field(center, around, offset):
        height = center.shape[2]
        extended = with_halo(center, (("gx", 0), ("gy", 1)), 3, False)
        extended = fix_edges(extended, 0, start_x, end_x, cells_x)
        extended = fix_edges(extended, 1, start_y, end_y, cells_y)
        x_shifted = [
            extended[3 + displace : 3 + displace + cells_x, 3 : 3 + cells_y]
            for displace in range(-3, 4)
        ]
        y_shifted = [
            extended[3 : 3 + cells_x, 3 + displace : 3 + displace + cells_y]
            for displace in range(-3, 4)
        ]
        head_shifted = [
            around[:, :, 3 + displace : 3 + displace + height] for displace in range(-3, 4)
        ]
        cos_head, sin_head = headings(offset, height)
        return hamilton(
            weno_pair(x_shifted, CELL_SIZE),
            weno_pair(y_shifted, CELL_SIZE),
            weno_pair(head_shifted, d_theta),
            weno_pair(speed_shifts(center), d_speed),
            cos_head,
            sin_head,
            speeds,
            wind_x,
            wind_y,
        )

    def around_heads(surface):
        return with_halo(surface, (("ha", 2),), 3, True)

    section_one = level_set + time_step * slope_field(level_set, around_heads(level_set), 0)
    section_two = 0.75 * level_set + 0.25 * (
        section_one + time_step * slope_field(section_one, around_heads(section_one), 0)
    )
    advanced = 1.0 / 3.0 * level_set + 2.0 / 3.0 * (
        section_two + time_step * slope_field(section_two, around_heads(section_two), 0)
    )
    return advanced - level_set


def solution(mesh):
    return jax.shard_map(
        body,
        mesh=mesh,
        in_specs=(P("gx", "gy", "ha", None), P(None, "gx", "gy")),
        out_specs=P("gx", "gy", "ha", None),
        check_vma=False,
    )
```

profile of v0, /device:TPU:0, one launch (start us, length us, event | category | flops | bytes accessed | tf_op | source)
XLA Modules:
  0.0 161.7 jit_solution(9486974208186733224)
XLA Ops:
  0.0 1.8 %fusion.560 = (f32[8,16,3,128]{3,1,2,0:T(8,128)S(1)}, f32[8,16,3,128]{3,1,2,0:T(8,128)}) fusion(f32[8,16,10,128]{3,1,2,0:T(8,128)} %param.2), kind=kLoop, calls=%fused_computation.890 | loop fusion | bytes 786432 | tf_op jit(solution)/shard_map/slice | solution.py:22
  1.8 3.1 %collective-permute-start.4 = (f32[8,16,3,128]{3,1,2,0:T(8,128)S(1)}, f32[8,16,3,128]{3,1,2,0:T(8,128)S(1)}, u32[]{:S(2)}, u32[]{:S(2)}) collective-permute-start(f32[8,16,3,128]{3,1,2,0:T(8,128)S(1)} %get-tuple-element.108), channel_id=1, source_target_pairs={{0,1},{1,2},{2,3},{3,0},{4,5},{5,6},{6,7},{7,4},{8,9},{9,10},{10,1... | collective-permute-start | bytes 589832 | tf_op jit(solution)/shard_map/ppermute | solution.py:25
  4.9 2.0 %collective-permute-start.5 = (f32[8,16,3,128]{3,1,2,0:T(8,128)}, f32[8,16,3,128]{3,1,2,0:T(8,128)}, u32[]{:S(2)}, u32[]{:S(2)}) collective-permute-start(f32[8,16,3,128]{3,1,2,0:T(8,128)} %get-tuple-element.109), channel_id=1, source_target_pairs={{1,0},{2,1},{3,2},{0,3},{5,4},{6,5},{7,6},{4,7},{9,8},{10,9},{11,1... | collective-permute-start | bytes 589832 | tf_op jit(solution)/shard_map/ppermute | solution.py:27
  6.9 1.8 %fusion.559 = (f32[3,16,10,128]{3,1,2,0:T(8,128)}, f32[3,16,10,128]{3,1,2,0:T(8,128)S(1)}) fusion(f32[8,16,10,128]{3,1,2,0:T(8,128)} %param.2), kind=kLoop, calls=%fused_computation.889 | loop fusion | bytes 983040 | tf_op jit(solution)/shard_map/slice | solution.py:21
  10.0 4.6 %collective-permute-start = (f32[3,16,10,128]{3,1,2,0:T(8,128)S(1)}, f32[3,16,10,128]{3,1,2,0:T(8,128)S(1)}, u32[]{:S(2)}, u32[]{:S(2)}) collective-permute-start(f32[3,16,10,128]{3,1,2,0:T(8,128)S(1)} %get-tuple-element.104), channel_id=1, source_target_pairs={{0,8},{8,16},{16,24},{1,9},{9,17},{17,25},{2,10},{10,18},{18,26},{... | collective-permute-start | bytes 737288 | tf_op jit(solution)/shard_map/ppermute | solution.py:25
  18.5 2.5 %multiply_add_fusion.28 = (f32[8,16,10,1]{3,1,2,0:T(8,128)}, f32[8,16,10,1]{3,1,2,0:T(8,128)}, f32[8,16,10,1]{3,1,2,0:T(8,128)}, f32[8,16,10,1]{3,1,2,0:T(8,128)...) fusion(f32[8,16,10,128]{3,1,2,0:T(8,128)S(1)} %copy-done), kind=kLoop, calls=%fused_computation.658 | loop fusion | flops 15360 | bytes 51200 | tf_op jit(solution)/shard_map/add | solution.py:45
  27.8 4.5 %collective-permute-start.2 = (f32[14,3,10,128]{3,0,2,1:T(8,128)}, f32[14,3,10,128]{3,0,2,1:T(8,128)}, u32[]{:S(2)}, u32[]{:S(2)}) collective-permute-start(f32[14,3,10,128]{3,0,2,1:T(8,128)} %copy.175), channel_id=1, source_target_pairs={{0,4},{1,5},{2,6},{3,7},{8,12},{9,13},{10,14},{11,15},{16,20},{17,... | collective-permute-start | bytes 645128 | tf_op jit(solution)/shard_map/ppermute | solution.py:25
  32.4 12.9 %pmax.7 = f32[]{:T(128)} all-reduce(f32[]{:T(128)} %fusion.530), channel_id=1, replica_groups=mesh['gx'=4,'gy'=2,'ha'=4] {'gx','gy'}, use_global_device_ids=true, to_apply=%region_1.0 | all-reduce | flops 1 | bytes 8 | tf_op jit(solution)/shard_map/pmax | solution.py:167
  53.5 17.6 %fusion.24 = f32[8,16,10,128]{3,1,2,0:T(8,128)S(1)} fusion(f32[8,16,10,128]{3,1,2,0:T(8,128)S(1)} %copy-done, f32[8,16,10,1]{3,1,2,0:T(8,128)S(1)} %copy-done.11, f32[8,16,10,1]{3,1,2,0:T(8,128)S(1)} %copy-done.9, f32[8,16,10,1]{3,1,2,0:T(8,128)S(1)} %copy-done.12, f32[8,16,10,125]{3,1,2,0:T(8,128)S(1)} %copy-done.6, f32[8,16,10,126]{3,1,2,0:T(8,128)S(1)} %copy-done.4, ...), kind=kLoop, calls=%fused_computation.102 | loop fusion | flops 99123200 | bytes 12309508 | tf_op jit(solution)/shard_map/add | solution.py:202
  72.2 3.8 %collective-permute-start.11 = (f32[8,16,3,128]{3,1,2,0:T(8,128)S(1)}, f32[8,16,3,128]{3,1,2,0:T(8,128)S(1)}, u32[]{:S(2)}, u32[]{:S(2)}) collective-permute-start(f32[8,16,3,128]{3,1,2,0:T(8,128)S(1)} %get-tuple-element.90), channel_id=1, source_target_pairs={{1,0},{2,1},{3,2},{0,3},{5,4},{6,5},{7,6},{4,7},{9,8},{10,9},{11,1... | collective-permute-start | bytes 589832 | tf_op jit(solution)/shard_map/ppermute | solution.py:27
  76.0 2.3 %collective-permute-start.6 = (f32[3,16,10,128]{3,1,2,0:T(8,128)S(1)}, f32[3,16,10,128]{3,1,2,0:T(8,128)S(1)}, u32[]{:S(2)}, u32[]{:S(2)}) collective-permute-start(f32[3,16,10,128]{3,1,2,0:T(8,128)S(1)} %get-tuple-element.87), channel_id=1, source_target_pairs={{0,8},{8,16},{16,24},{1,9},{9,17},{17,25},{2,10},{10,18},{18,26},{... | collective-permute-start | bytes 737288 | tf_op jit(solution)/shard_map/ppermute | solution.py:25
  78.3 1.3 collective-permute-start.7
  79.9 3.2 %collective-permute-done.6 = f32[3,16,10,128]{3,1,2,0:T(8,128)S(1)} collective-permute-done((f32[3,16,10,128]{3,1,2,0:T(8,128)S(1)}, f32[3,16,10,128]{3,1,2,0:T(8,128)S(1)}, u32[]{:S(2)}, u32[]{:S(2)}) %collective-permute-start.6) | collective-permute-done | bytes 245792 | tf_op jit(solution)/shard_map/ppermute | solution.py:25
  83.1 8.6 %collective-permute-done.7 = f32[3,16,10,128]{3,1,2,0:T(8,128)S(1)} collective-permute-done((f32[3,16,10,128]{3,1,2,0:T(8,128)S(1)}, f32[3,16,10,128]{3,1,2,0:T(8,128)S(1)}, u32[]{:S(2)}, u32[]{:S(2)}) %collective-permute-start.7) | collective-permute-done | bytes 245792 | tf_op jit(solution)/shard_map/ppermute | solution.py:27
  92.0 1.3 collective-permute-start.9
  93.3 3.2 %collective-permute-start.8 = (f32[14,3,10,128]{3,0,2,1:T(8,128)S(1)}, f32[14,3,10,128]{3,0,2,1:T(8,128)S(1)}, u32[]{:S(2)}, u32[]{:S(2)}) collective-permute-start(f32[14,3,10,128]{3,0,2,1:T(8,128)S(1)} %copy.179), channel_id=1, source_target_pairs={{0,4},{1,5},{2,6},{3,7},{8,12},{9,13},{10,14},{11,15},{16,20},{17,... | collective-permute-start | bytes 645128 | tf_op jit(solution)/shard_map/ppermute | solution.py:25
  99.6 17.6 %fusion.35 = f32[8,16,10,128]{3,1,2,0:T(8,128)S(1)} fusion(f32[8,16,10,128]{3,1,2,0:T(8,128)S(1)} %fusion.24, f32[8,16,10,1]{3,1,2,0:T(8,128)S(1)} %get-tuple-element.96, f32[8,16,10,1]{3,1,2,0:T(8,128)S(1)} %get-tuple-element.100, f32[8,16,10,1]{3,1,2,0:T(8,128)S(1)} %get-tuple-element.97, f32[8,16,10,125]{3,1,2,0:T(8,128)S(1)} %get-tuple-element.102, ...), kind=kLoop, calls=%fused_computation.113 | loop fusion | flops 100597760 | bytes 9425924 | tf_op jit(solution)/shard_map/add | solution.py:203
  118.2 3.8 %collective-permute-start.17 = (f32[8,16,3,128]{3,1,2,0:T(8,128)S(1)}, f32[8,16,3,128]{3,1,2,0:T(8,128)S(1)}, u32[]{:S(2)}, u32[]{:S(2)}) collective-permute-start(f32[8,16,3,128]{3,1,2,0:T(8,128)S(1)} %get-tuple-element.74), channel_id=1, source_target_pairs={{1,0},{2,1},{3,2},{0,3},{5,4},{6,5},{7,6},{4,7},{9,8},{10,9},{11,1... | collective-permute-start | bytes 589832 | tf_op jit(solution)/shard_map/ppermute | solution.py:27
  122.0 2.2 %collective-permute-start.12 = (f32[3,16,10,128]{3,1,2,0:T(8,128)S(1)}, f32[3,16,10,128]{3,1,2,0:T(8,128)S(1)}, u32[]{:S(2)}, u32[]{:S(2)}) collective-permute-start(f32[3,16,10,128]{3,1,2,0:T(8,128)S(1)} %get-tuple-element.71), channel_id=1, source_target_pairs={{0,8},{8,16},{16,24},{1,9},{9,17},{17,25},{2,10},{10,18},{18,26},{... | collective-permute-start | bytes 737288 | tf_op jit(solution)/shard_map/ppermute | solution.py:25
  124.3 1.3 collective-permute-start.13
  125.8 3.6 %collective-permute-done.12 = f32[3,16,10,128]{3,1,2,0:T(8,128)S(1)} collective-permute-done((f32[3,16,10,128]{3,1,2,0:T(8,128)S(1)}, f32[3,16,10,128]{3,1,2,0:T(8,128)S(1)}, u32[]{:S(2)}, u32[]{:S(2)}) %collective-permute-start.12) | collective-permute-done | bytes 245792 | tf_op jit(solution)/shard_map/ppermute | solution.py:25
  129.4 6.0 %collective-permute-done.13 = f32[3,16,10,128]{3,1,2,0:T(8,128)S(1)} collective-permute-done((f32[3,16,10,128]{3,1,2,0:T(8,128)S(1)}, f32[3,16,10,128]{3,1,2,0:T(8,128)S(1)}, u32[]{:S(2)}, u32[]{:S(2)}) %collective-permute-start.13) | collective-permute-done | bytes 245792 | tf_op jit(solution)/shard_map/ppermute | solution.py:27
  136.9 3.1 %collective-permute-start.14 = (f32[14,3,10,128]{3,0,2,1:T(8,128)S(1)}, f32[14,3,10,128]{3,0,2,1:T(8,128)S(1)}, u32[]{:S(2)}, u32[]{:S(2)}) collective-permute-start(f32[14,3,10,128]{3,0,2,1:T(8,128)S(1)} %copy.183), channel_id=1, source_target_pairs={{0,4},{1,5},{2,6},{3,7},{8,12},{9,13},{10,14},{11,15},{16,20},{17,... | collective-permute-start | bytes 645128 | tf_op jit(solution)/shard_map/ppermute | solution.py:25
  143.3 18.4 %fusion.47 = f32[8,16,10,128]{3,1,2,0:T(8,128)} fusion(f32[8,16,10,128]{3,1,2,0:T(8,128)S(1)} %copy-done, f32[8,16,10,128]{3,1,2,0:T(8,128)S(1)} %fusion.35, f32[8,16,10,1]{3,1,2,0:T(8,128)S(1)} %get-tuple-element.80, f32[8,16,10,1]{3,1,2,0:T(8,128)S(1)} %get-tuple-element.84, f32[8,16,10,1]{3,1,2,0:T(8,128)S(1)} %get-tuple-element.81, ...), kind=kLoop, calls=%fused_computation.125 | loop fusion | flops 100761600 | bytes 9425924 | tf_op jit(solution)/shard_map/sub | solution.py:209
  (130 shorter events, 29.7 us)
Async XLA Ops:
  0.0 14.6 %copy-start = (f32[8,16,10,128]{3,1,2,0:T(8,128)S(1)}, f32[8,16,10,128]{3,1,2,0:T(8,128)}, u32[]{:S(2)}) copy-start(f32[8,16,10,128]{3,1,2,0:T(8,128)} %param.2) | copy-start | bytes 1966084
  1.8 21.9 %collective-permute-start.4 = (f32[8,16,3,128]{3,1,2,0:T(8,128)S(1)}, f32[8,16,3,128]{3,1,2,0:T(8,128)S(1)}, u32[]{:S(2)}, u32[]{:S(2)}) collective-permute-start(f32[8,16,3,128]{3,1,2,0:T(8,128)S(1)} %get-tuple-element.108), channel_id=1, source_target_pairs={{0,1},{1,2},{2,3},{3,0},{4,5},{5,6},{6,7},{7,4},{8,9},{9,10},{10,1... | collective-permute-start | bytes 589832 | tf_op jit(solution)/shard_map/ppermute | solution.py:25
  4.9 41.1 %collective-permute-start.5 = (f32[8,16,3,128]{3,1,2,0:T(8,128)}, f32[8,16,3,128]{3,1,2,0:T(8,128)}, u32[]{:S(2)}, u32[]{:S(2)}) collective-permute-start(f32[8,16,3,128]{3,1,2,0:T(8,128)} %get-tuple-element.109), channel_id=1, source_target_pairs={{1,0},{2,1},{3,2},{0,3},{5,4},{6,5},{7,6},{4,7},{9,8},{10,9},{11,1... | collective-permute-start | bytes 589832 | tf_op jit(solution)/shard_map/ppermute | solution.py:27
  8.7 15.2 %collective-permute-start.1 = (f32[3,16,10,128]{3,1,2,0:T(8,128)}, f32[3,16,10,128]{3,1,2,0:T(8,128)}, u32[]{:S(2)}, u32[]{:S(2)}) collective-permute-start(f32[3,16,10,128]{3,1,2,0:T(8,128)} %get-tuple-element.103), channel_id=1, source_target_pairs={{8,0},{16,8},{24,16},{9,1},{17,9},{25,17},{10,2},{18,10},{26,18},{... | collective-permute-start | bytes 737288 | tf_op jit(solution)/shard_map/ppermute | solution.py:27
  10.0 13.7 %collective-permute-start = (f32[3,16,10,128]{3,1,2,0:T(8,128)S(1)}, f32[3,16,10,128]{3,1,2,0:T(8,128)S(1)}, u32[]{:S(2)}, u32[]{:S(2)}) collective-permute-start(f32[3,16,10,128]{3,1,2,0:T(8,128)S(1)} %get-tuple-element.104), channel_id=1, source_target_pairs={{0,8},{8,16},{16,24},{1,9},{9,17},{17,25},{2,10},{10,18},{18,26},{... | collective-permute-start | bytes 737288 | tf_op jit(solution)/shard_map/ppermute | solution.py:25
  18.5 3.1 %copy-start.13 = (f32[2,8,16]{2,1,0:T(8,128)S(1)}, f32[2,8,16]{2,1,0:T(8,128)}, u32[]{:S(2)}) copy-start(f32[2,8,16]{2,1,0:T(8,128)} %param.3) | copy-start | bytes 3076
  26.5 20.4 %collective-permute-start.3 = (f32[14,3,10,128]{3,0,2,1:T(8,128)}, f32[14,3,10,128]{3,0,2,1:T(8,128)}, u32[]{:S(2)}, u32[]{:S(2)}) collective-permute-start(f32[14,3,10,128]{3,0,2,1:T(8,128)} %copy.176), channel_id=1, source_target_pairs={{4,0},{5,1},{6,2},{7,3},{12,8},{13,9},{14,10},{15,11},{20,16},{21,... | collective-permute-start | bytes 645128 | tf_op jit(solution)/shard_map/ppermute | solution.py:27
  27.8 20.2 %collective-permute-start.2 = (f32[14,3,10,128]{3,0,2,1:T(8,128)}, f32[14,3,10,128]{3,0,2,1:T(8,128)}, u32[]{:S(2)}, u32[]{:S(2)}) collective-permute-start(f32[14,3,10,128]{3,0,2,1:T(8,128)} %copy.175), channel_id=1, source_target_pairs={{0,4},{1,5},{2,6},{3,7},{8,12},{9,13},{10,14},{11,15},{16,20},{17,... | collective-permute-start | bytes 645128 | tf_op jit(solution)/shard_map/ppermute | solution.py:25
  50.5 2.4 %copy-start.2 = (f32[8,16,10,127]{3,1,2,0:T(8,128)S(1)}, f32[8,16,10,127]{3,1,2,0:T(8,128)}, u32[]{:S(2)}) copy-start(f32[8,16,10,127]{3,1,2,0:T(8,128)} %get-tuple-element.111) | copy-start | bytes 1950724
  50.5 2.6 %copy-start.3 = (f32[8,16,10,126]{3,1,2,0:T(8,128)S(1)}, f32[8,16,10,126]{3,1,2,0:T(8,128)}, u32[]{:S(2)}) copy-start(f32[8,16,10,126]{3,1,2,0:T(8,128)} %get-tuple-element.112) | copy-start | bytes 1935364
  50.5 2.8 %copy-start.4 = (f32[8,16,10,126]{3,1,2,0:T(8,128)S(1)}, f32[8,16,10,126]{3,1,2,0:T(8,128)}, u32[]{:S(2)}) copy-start(f32[8,16,10,126]{3,1,2,0:T(8,128)} %get-tuple-element.113) | copy-start | bytes 1935364
  50.5 2.9 %copy-start.5 = (f32[8,16,10,125]{3,1,2,0:T(8,128)S(1)}, f32[8,16,10,125]{3,1,2,0:T(8,128)}, u32[]{:S(2)}) copy-start(f32[8,16,10,125]{3,1,2,0:T(8,128)} %get-tuple-element.120) | copy-start | bytes 1920004
  72.1 27.5 %collective-permute-start.10 = (f32[8,16,3,128]{3,1,2,0:T(8,128)S(1)}, f32[8,16,3,128]{3,1,2,0:T(8,128)S(1)}, u32[]{:S(2)}, u32[]{:S(2)}) collective-permute-start(f32[8,16,3,128]{3,1,2,0:T(8,128)S(1)} %get-tuple-element.89), channel_id=1, source_target_pairs={{0,1},{1,2},{2,3},{3,0},{4,5},{5,6},{6,7},{7,4},{8,9},{9,10},{10,1... | collective-permute-start | bytes 589832 | tf_op jit(solution)/shard_map/ppermute | solution.py:25
  72.2 27.5 %collective-permute-start.11 = (f32[8,16,3,128]{3,1,2,0:T(8,128)S(1)}, f32[8,16,3,128]{3,1,2,0:T(8,128)S(1)}, u32[]{:S(2)}, u32[]{:S(2)}) collective-permute-start(f32[8,16,3,128]{3,1,2,0:T(8,128)S(1)} %get-tuple-element.90), channel_id=1, source_target_pairs={{1,0},{2,1},{3,2},{0,3},{5,4},{6,5},{7,6},{4,7},{9,8},{10,9},{11,1... | collective-permute-start | bytes 589832 | tf_op jit(solution)/shard_map/ppermute | solution.py:27
  76.0 7.1 %collective-permute-start.6 = (f32[3,16,10,128]{3,1,2,0:T(8,128)S(1)}, f32[3,16,10,128]{3,1,2,0:T(8,128)S(1)}, u32[]{:S(2)}, u32[]{:S(2)}) collective-permute-start(f32[3,16,10,128]{3,1,2,0:T(8,128)S(1)} %get-tuple-element.87), channel_id=1, source_target_pairs={{0,8},{8,16},{16,24},{1,9},{9,17},{17,25},{2,10},{10,18},{18,26},{... | collective-permute-start | bytes 737288 | tf_op jit(solution)/shard_map/ppermute | solution.py:25
  78.3 13.4 %collective-permute-start.7 = (f32[3,16,10,128]{3,1,2,0:T(8,128)S(1)}, f32[3,16,10,128]{3,1,2,0:T(8,128)S(1)}, u32[]{:S(2)}, u32[]{:S(2)}) collective-permute-start(f32[3,16,10,128]{3,1,2,0:T(8,128)S(1)} %get-tuple-element.88), channel_id=1, source_target_pairs={{8,0},{16,8},{24,16},{9,1},{17,9},{25,17},{10,2},{18,10},{26,18},{... | collective-permute-start | bytes 737288 | tf_op jit(solution)/shard_map/ppermute | solution.py:27
  92.0 4.8 %collective-permute-start.9 = (f32[14,3,10,128]{3,0,2,1:T(8,128)S(1)}, f32[14,3,10,128]{3,0,2,1:T(8,128)S(1)}, u32[]{:S(2)}, u32[]{:S(2)}) collective-permute-start(f32[14,3,10,128]{3,0,2,1:T(8,128)S(1)} %copy.180), channel_id=1, source_target_pairs={{4,0},{5,1},{6,2},{7,3},{12,8},{13,9},{14,10},{15,11},{20,16},{21,... | collective-permute-start | bytes 645128 | tf_op jit(solution)/shard_map/ppermute | solution.py:27
  93.3 4.2 %collective-permute-start.8 = (f32[14,3,10,128]{3,0,2,1:T(8,128)S(1)}, f32[14,3,10,128]{3,0,2,1:T(8,128)S(1)}, u32[]{:S(2)}, u32[]{:S(2)}) collective-permute-start(f32[14,3,10,128]{3,0,2,1:T(8,128)S(1)} %copy.179), channel_id=1, source_target_pairs={{0,4},{1,5},{2,6},{3,7},{8,12},{9,13},{10,14},{11,15},{16,20},{17,... | collective-permute-start | bytes 645128 | tf_op jit(solution)/shard_map/ppermute | solution.py:25
  118.2 25.1 %collective-permute-start.16 = (f32[8,16,3,128]{3,1,2,0:T(8,128)S(1)}, f32[8,16,3,128]{3,1,2,0:T(8,128)S(1)}, u32[]{:S(2)}, u32[]{:S(2)}) collective-permute-start(f32[8,16,3,128]{3,1,2,0:T(8,128)S(1)} %get-tuple-element.73), channel_id=1, source_target_pairs={{0,1},{1,2},{2,3},{3,0},{4,5},{5,6},{6,7},{7,4},{8,9},{9,10},{10,1... | collective-permute-start | bytes 589832 | tf_op jit(solution)/shard_map/ppermute | solution.py:25
  118.2 25.1 %collective-permute-start.17 = (f32[8,16,3,128]{3,1,2,0:T(8,128)S(1)}, f32[8,16,3,128]{3,1,2,0:T(8,128)S(1)}, u32[]{:S(2)}, u32[]{:S(2)}) collective-permute-start(f32[8,16,3,128]{3,1,2,0:T(8,128)S(1)} %get-tuple-element.74), channel_id=1, source_target_pairs={{1,0},{2,1},{3,2},{0,3},{5,4},{6,5},{7,6},{4,7},{9,8},{10,9},{11,1... | collective-permute-start | bytes 589832 | tf_op jit(solution)/shard_map/ppermute | solution.py:27
  122.0 7.4 %collective-permute-start.12 = (f32[3,16,10,128]{3,1,2,0:T(8,128)S(1)}, f32[3,16,10,128]{3,1,2,0:T(8,128)S(1)}, u32[]{:S(2)}, u32[]{:S(2)}) collective-permute-start(f32[3,16,10,128]{3,1,2,0:T(8,128)S(1)} %get-tuple-element.71), channel_id=1, source_target_pairs={{0,8},{8,16},{16,24},{1,9},{9,17},{17,25},{2,10},{10,18},{18,26},{... | collective-permute-start | bytes 737288 | tf_op jit(solution)/shard_map/ppermute | solution.py:25
  124.3 11.2 %collective-permute-start.13 = (f32[3,16,10,128]{3,1,2,0:T(8,128)S(1)}, f32[3,16,10,128]{3,1,2,0:T(8,128)S(1)}, u32[]{:S(2)}, u32[]{:S(2)}) collective-permute-start(f32[3,16,10,128]{3,1,2,0:T(8,128)S(1)} %get-tuple-element.72), channel_id=1, source_target_pairs={{8,0},{16,8},{24,16},{9,1},{17,9},{25,17},{10,2},{18,10},{26,18},{... | collective-permute-start | bytes 737288 | tf_op jit(solution)/shard_map/ppermute | solution.py:27
  135.6 4.6 %collective-permute-start.15 = (f32[14,3,10,128]{3,0,2,1:T(8,128)S(1)}, f32[14,3,10,128]{3,0,2,1:T(8,128)S(1)}, u32[]{:S(2)}, u32[]{:S(2)}) collective-permute-start(f32[14,3,10,128]{3,0,2,1:T(8,128)S(1)} %copy.184), channel_id=1, source_target_pairs={{4,0},{5,1},{6,2},{7,3},{12,8},{13,9},{14,10},{15,11},{20,16},{21,... | collective-permute-start | bytes 645128 | tf_op jit(solution)/shard_map/ppermute | solution.py:27
  136.9 4.2 %collective-permute-start.14 = (f32[14,3,10,128]{3,0,2,1:T(8,128)S(1)}, f32[14,3,10,128]{3,0,2,1:T(8,128)S(1)}, u32[]{:S(2)}, u32[]{:S(2)}) collective-permute-start(f32[14,3,10,128]{3,0,2,1:T(8,128)S(1)} %copy.183), channel_id=1, source_target_pairs={{0,4},{1,5},{2,6},{3,7},{8,12},{9,13},{10,14},{11,15},{16,20},{17,... | collective-permute-start | bytes 645128 | tf_op jit(solution)/shard_map/ppermute | solution.py:25
  (8 other events, 13.6 us)
where the time goes:
time: 162 us
  other arithmetic  65.1 us (40%)
  starting transfers between devices  40.4 us (25%)
  waiting for transfers between devices  22.8 us (14%)
  local copies, waits for them, and re-layouts  19.1 us (12%)
  blocking collectives  12.9 us (8%)
    ppermute x9, starting transfers between devices, with_halo(): lax.ppermute(tail, axis, [(i, (i + 1) % count) for i in range(ends)])  23 us
    sub x1, other arithmetic, body(): return advanced - level_set  18.4 us
    add x1, other arithmetic, body(): level_set + time_step * slope_field(level_set, around_heads(level_set), 0)  17.6 us
    add x1, other arithmetic, body(): 0.75 * level_set  17.6 us
    ppermute x9, starting transfers between devices, with_halo(): lax.ppermute(head, axis, [((i + 1) % count, i) for i in range(ends)])  17.4 us
    ppermute x9, waiting for transfers between devices, with_halo(): lax.ppermute(head, axis, [((i + 1) % count, i) for i in range(ends)])  14.7 us
    pmax x1, blocking collectives, body(): top_rate = lax.pmax(local_top, ('gx', 'gy'))  12.9 us
    ppermute x9, waiting for transfers between devices, with_halo(): lax.ppermute(tail, axis, [(i, (i + 1) % count) for i in range(ends)])  8.09 us
  transfers between devices with their start and end apart: 18, of which 6 were waited for; matrix products, arithmetic and copies ran while one was open for 13% of the time, Pallas kernels for 0%

commit v1 on v0

v1 whole, which is shorter than its diff:
```python
import functools
import math

import jax
import jax.numpy as jnp
import numpy as np
from jax import lax
from jax.experimental import pallas as pl
from jax.experimental.pallas import tpu as pltpu
from jax.sharding import PartitionSpec as P

CELL_SIZE = 0.05
SPEED_LOW = 0.1
SPEED_SPAN = 0.4
TURN_MAX = 1.0
ACCEL_MAX = 0.05
CFL_NUMBER = 0.5
WENO_EPS = 1e-06
SCALE = 32.0
PAD = 8
MESH = pl.DeviceIdType.MESH


def rcp(d):
    x = pl.reciprocal(d, approx=True)
    return x * (2.0 - d * x)


def eps_of(spacing):
    return 0.75 * WENO_EPS * (spacing * SCALE) ** 2


def upwind(dm2, dm1, d0, dp1, dp2, c0, c1, fh, eps):
    pos = fh > 0.0
    d1 = jnp.where(pos, dp2, dm2)
    d2 = jnp.where(pos, dp1, dm1)
    d4 = jnp.where(pos, dm1, dp1)
    c = jnp.where(pos, c1, c0)
    d3 = d0
    e1 = d2 - d1
    e2 = d3 - d2
    e3 = d4 - d3
    g2 = 0.75 * d2
    g3 = 0.75 * d3
    s1 = e1 * e1 + (g2 * (d2 + e1) + eps)
    s2 = e2 * e2 + (g2 * d3 + eps)
    s3 = e3 * e3 + (g3 * (d3 - e3) + eps)
    t1 = s2 * s3
    t2 = s1 * s3
    t3 = s1 * s2
    r1 = t1 * t1
    r2 = t2 * t2
    w3 = 1.5 * (t3 * t3)
    num = r1 * (e1 - e2) + w3 * (e2 - e3)
    den = (r1 + 6.0 * r2) + (w3 + w3)
    q = (d3 + 0.5 * d2) + num * rcp(den)
    return q * (jnp.abs(fh) * (1.0 / 3.0)) - c * fh


def triple(da, db, eps):
    e = db - da
    s2 = e * e + (0.75 * (da * db) + eps)
    h = 1.5 * e
    return e, s2 + db * h, s2, s2 - da * h


def face_pair(c, d2, d3, e1, e2, e3, s1, s2, s3):
    t1 = s2 * s3
    t2 = s1 * s3
    t3 = s1 * s2
    r1 = t1 * t1
    r2 = t2 * t2
    r3 = t3 * t3
    a = r1 * (e1 - e2)
    b = r3 * (e2 - e3)
    m = 6.0 * r2 + (r1 + r3)
    n = a + b
    left = (3.0 * c + (d3 + 0.5 * d2)) + (n + 0.5 * b) * rcp(m + (r3 + r3))
    right = ((d2 + 0.5 * d3) - 3.0 * c) + (n + 0.5 * a) * rcp(m + (r1 + r1))
    return left, right


def kernel(sizes, axes, u_ref, wind_ref, flow_ref, rate_ref, out_ref,
           b0, b1, b2, acc, wind, best, peers, step, sends, recvs, rsend, rrecv):
    nx, ny, nh, nv = sizes
    ngx, ngy, nha = axes
    bufs = (b0, b1, b2)
    d_theta = 2.0 * math.pi / (nh * nha)
    d_speed = SPEED_SPAN / nv
    tiles = ny // 8
    gx, gy, ha = lax.axis_index("gx"), lax.axis_index("gy"), lax.axis_index("ha")
    n_xy = ngx * ngy
    me = gx * ngy + gy

    def peer(delta):
        other = lax.rem(me + delta, n_xy)
        return {"gx": other // ngy, "gy": lax.rem(other, ngy)}

    up_ha = {"ha": lax.rem(ha + 1, nha)}
    down_ha = {"ha": lax.rem(ha + nha - 1, nha)}
    barrier = pltpu.get_barrier_semaphore()
    for delta in range(1, n_xy):
        pl.semaphore_signal(barrier, inc=1, device_id=peer(delta), device_id_type=MESH)
    for target in (up_ha, down_ha):
        pl.semaphore_signal(barrier, inc=1, device_id=target, device_id_type=MESH)

    def load_plane(x, carry):
        for k in range(nh):
            b0[3 + x, 3 + k, PAD:PAD + ny, :] = u_ref[x, k] * SCALE
        for comp in range(2):
            for y in range(ny):
                wind[comp, x, y:y + 1, :] = jnp.full((1, nv), wind_ref[comp, x, y], jnp.float32)
        return carry

    lax.fori_loop(0, nx, load_plane, 0)

    def rate_plane(x, top):
        for r in range(rate_ref.shape[1]):
            for t in range(tiles):
                fx = rate_ref[0, r:r + 1, :] + wind[0, x, 8 * t:8 * t + 8, :]
                fy = rate_ref[1, r:r + 1, :] + wind[1, x, 8 * t:8 * t + 8, :]
                top = jnp.maximum(top, (jnp.abs(fx) + jnp.abs(fy)) * (1.0 / CELL_SIZE))
        return top

    best[...] = lax.fori_loop(0, nx, rate_plane, jnp.zeros((8, 128), jnp.float32))

    pl.semaphore_wait(barrier, n_xy + 1)

    xs, hs, ys = pl.ds(3, nx), pl.ds(3, nh), pl.ds(PAD, ny)

    def copies(s):
        buf = bufs[s]
        plans = (
            (buf.at[pl.ds(nx, 3), hs, ys], buf.at[pl.ds(0, 3), hs, ys], {"gx": gx + 1},
             gx < ngx - 1, gx > 0),
            (buf.at[pl.ds(3, 3), hs, ys], buf.at[pl.ds(3 + nx, 3), hs, ys], {"gx": gx - 1},
             gx > 0, gx < ngx - 1),
            (buf.at[xs, pl.ds(nh, 3), ys], buf.at[xs, pl.ds(0, 3), ys], up_ha, None, None),
            (buf.at[xs, pl.ds(3, 3), ys], buf.at[xs, pl.ds(3 + nh, 3), ys], down_ha, None, None),
            (buf.at[xs, hs, pl.ds(ny, PAD)], buf.at[xs, hs, pl.ds(0, PAD)], {"gy": gy + 1},
             gy < ngy - 1, gy > 0),
            (buf.at[xs, hs, pl.ds(PAD, PAD)], buf.at[xs, hs, pl.ds(PAD + ny, PAD)], {"gy": gy - 1},
             gy > 0, gy < ngy - 1),
        )
        return [
            (pltpu.make_async_remote_copy(
                src_ref=src, dst_ref=dst, send_sem=sends.at[s, i], recv_sem=recvs.at[s, i],
                device_id=target, device_id_type=MESH), has_out, has_in)
            for i, (src, dst, target, has_out, has_in) in enumerate(plans)
        ]

    def under(condition, act):
        if condition is None:
            act()
        else:
            pl.when(condition)(act)

    rate_copies = [
        pltpu.make_async_remote_copy(
            src_ref=best, dst_ref=peers.at[delta - 1], send_sem=rsend.at[delta - 1],
            recv_sem=rrecv.at[delta - 1], device_id=peer(delta), device_id_type=MESH)
        for delta in range(1, n_xy)
    ]
    plans = [copies(s) for s in range(3)]

    def send_all(s):
        for copy, has_out, _ in plans[s]:
            under(has_out, copy.start)

    def wait_in(s, which):
        for i in which:
            copy, _, has_in = plans[s][i]
            under(has_in, copy.wait_recv)

    def v_pass(buf):
        eps = eps_of(d_speed)
        coef = ACCEL_MAX / (3.0 * d_speed)
        e4 = np.float32(np.float32(eps * eps) ** 2)
        edge = lax.broadcasted_iota(jnp.int32, (ny, nv), 1) == 0

        def one(u):
            up = lambda a: pltpu.roll(a, 1, 1)
            down = lambda a: pltpu.roll(a, nv - 1, 1)
            q = u - up(u)
            q = jnp.where(edge, down(q), q)
            qm = up(q)
            d = jnp.where(edge, 0.0, q - qm)
            d3 = down(d)
            e2, f1, s2, f3 = triple(d, d3, eps)
            e1, e3, s1, s3 = up(e2), down(e2), up(f1), down(f3)
            t1 = s2 * s3
            t2 = s1 * s3
            t3 = s1 * s2
            r1 = t1 * t1
            r2 = t2 * t2
            r3 = t3 * t3
            f12 = e1 - e2
            f23 = e2 - e3
            r2l = jnp.where(edge, r1, r2)
            r3l = jnp.where(edge, e4, r3)
            r2r = jnp.where(edge, r3, r2)
            r1r = jnp.where(edge, e4, r1)
            al = r1 * jnp.where(edge, 0.0, f12)
            bl = r3l * f23
            ar = r1r * f12
            br = r3 * jnp.where(edge, 0.0, f23)
            cr = jnp.where(edge, qm, q)
            left = (3.0 * q + (d3 + 0.5 * d)) + (al + 1.5 * bl) * rcp(r1 + 6.0 * r2l + 3.0 * r3l)
            right = ((d + 0.5 * d3) - 3.0 * cr) + (1.5 * ar + br) * rcp(3.0 * r1r + 6.0 * r2r + r3)
            return coef * jnp.minimum(left, down(right))

        def body(x, carry):
            def inner(k, carry):
                for j in range(2):
                    acc[x, 2 * k + j] = one(buf[3 + x, 3 + 2 * k + j, PAD:PAD + ny, :])
                return carry
            return lax.fori_loop(0, nh // 2, inner, carry)

        lax.fori_loop(0, nx, body, 0)

    def h_pass(buf):
        eps = eps_of(d_theta)
        coef = TURN_MAX / (3.0 * d_theta)

        def body(i, carry):
            x = i // tiles
            rows = pl.ds(pl.multiple_of(lax.rem(i, tiles) * 8, 8) + PAD, 8)
            rows_acc = pl.ds(pl.multiple_of(lax.rem(i, tiles) * 8, 8), 8)
            u = [buf[3 + x, j, rows, :] for j in range(nh + 6)]
            q = [u[j + 1] - u[j] for j in range(nh + 5)]
            d = [q[j + 1] - q[j] for j in range(nh + 4)]
            tr = [triple(d[j], d[j + 1], eps) for j in range(nh + 3)]
            before = None
            for f in range(nh + 1):
                left, right = face_pair(
                    q[f + 2], d[f + 1], d[f + 2], tr[f][0], tr[f + 1][0], tr[f + 2][0],
                    tr[f][1], tr[f + 1][2], tr[f + 2][3])
                if before is not None:
                    acc[x, f - 1, rows_acc, :] += coef * jnp.minimum(before, right)
                before = left
            return carry

        lax.fori_loop(0, nx * tiles, body, 0)

    def flow_row(comp, k):
        return flow_ref[comp, pl.ds(ha * nh + k, 1), :]

    def y_pass(buf):
        eps = eps_of(CELL_SIZE)

        def body(x, carry):
            def inner(k, carry):
                row = flow_row(1, k)
                for t in range(tiles):
                    u = [buf[3 + x, 3 + k, PAD + 8 * t + j:PAD + 8 * t + j + 8, :] for j in range(-3, 4)]
                    q = [u[j + 1] - u[j] for j in range(6)]
                    d = [q[j + 1] - q[j] for j in range(5)]
                    fh = (row + wind[1, x, 8 * t:8 * t + 8, :]) * (1.0 / CELL_SIZE)
                    acc[x, k, 8 * t:8 * t + 8, :] += upwind(*d, q[2], q[3], fh, eps)
                return carry
            return lax.fori_loop(0, nh, inner, carry)

        lax.fori_loop(0, nx, body, 0)

    def x_pass(s):
        buf = bufs[s]
        eps = eps_of(CELL_SIZE)

        def body(i, carry):
            k = i // tiles
            base = pl.multiple_of(lax.rem(i, tiles) * 8, 8)
            rows, rows_acc = pl.ds(base + PAD, 8), pl.ds(base, 8)
            row = flow_row(0, k)
            dt = step[...]
            u = [buf[j, 3 + k, rows, :] for j in range(nx + 6)]
            q = [u[j + 1] - u[j] for j in range(nx + 5)]
            d = [q[j + 1] - q[j] for j in range(nx + 4)]
            for x in range(nx):
                fh = (row + wind[0, x, rows_acc, :]) * (1.0 / CELL_SIZE)
                total = acc[x, k, rows_acc, :] + upwind(*d[x:x + 5], q[x + 2], q[x + 3], fh, eps)
                moved = u[x + 3] - dt * jnp.maximum(total, 0.0)
                if s == 0:
                    b1[3 + x, 3 + k, rows, :] = moved
                elif s == 1:
                    b2[3 + x, 3 + k, rows, :] = 0.75 * b0[3 + x, 3 + k, rows, :] + 0.25 * moved
                else:
                    out_ref[x, k, rows_acc, :] = (moved - b0[3 + x, 3 + k, rows, :]) * (2.0 / (3.0 * SCALE))
            return carry

        lax.fori_loop(0, nh * tiles, body, 0)

    def fill_x(buf):
        def ends(low):
            def act():
                def body(k, carry):
                    edge = buf[3 if low else nx + 2, 3 + k, PAD:PAD + ny, :]
                    slope = edge - buf[4 if low else nx + 1, 3 + k, PAD:PAD + ny, :]
                    for r in range(1, 4):
                        buf[3 - r if low else nx + 2 + r, 3 + k, PAD:PAD + ny, :] = edge + r * slope
                    return carry
                lax.fori_loop(0, nh, body, 0)
            return act
        pl.when(gx == 0)(ends(True))
        pl.when(gx == ngx - 1)(ends(False))

    def fill_y(buf):
        index = lax.broadcasted_iota(jnp.int32, (8, nv), 0).astype(jnp.float32)

        def ends(low):
            reach = (8.0 - index) if low else (index + 1.0)
            at, near, to = (PAD, PAD + 1, 0) if low else (PAD + ny - 1, PAD + ny - 2, PAD + ny)

            def act():
                def body(x, carry):
                    def inner(k, carry):
                        edge = buf[3 + x, 3 + k, at:at + 1, :]
                        slope = edge - buf[3 + x, 3 + k, near:near + 1, :]
                        buf[3 + x, 3 + k, to:to + 8, :] = edge + reach * slope
                        return carry
                    return lax.fori_loop(0, nh, inner, carry)
                lax.fori_loop(0, nx, body, 0)
            return act
        pl.when(gy == 0)(ends(True))
        pl.when(gy == ngy - 1)(ends(False))

    for s in range(3):
        send_all(s)
        if s == 0:
            for copy in rate_copies:
                copy.start()
        v_pass(bufs[s])
        fill_y(bufs[s])
        fill_x(bufs[s])
        wait_in(s, (4, 5))
        y_pass(bufs[s])
        wait_in(s, (2, 3))
        h_pass(bufs[s])
        if s == 0:
            for copy in rate_copies:
                copy.wait_recv()
            top = best[...]
            for delta in range(1, n_xy):
                top = jnp.maximum(top, peers[delta - 1])
            rate = jnp.max(top, axis=(0, 1), keepdims=True) + (TURN_MAX / d_theta + ACCEL_MAX / d_speed)
            step[...] = jnp.broadcast_to(CFL_NUMBER / rate, step.shape)
        wait_in(s, (0, 1))
        x_pass(s)

    for copy in rate_copies:
        copy.wait_send()
    for s in range(3):
        for copy, has_out, _ in plans[s]:
            under(has_out, copy.wait_send)


def tables(nv, n_head):
    speeds = (SPEED_LOW + SPEED_SPAN * (np.arange(nv, dtype=np.float32) + np.float32(0.5)) / nv).astype(np.float32)
    angles = np.arange(n_head, dtype=np.float32) * np.float32(2.0 * math.pi / n_head)
    turns = np.stack([np.cos(angles.astype(np.float64)), np.sin(angles.astype(np.float64))]).astype(np.float32)
    flow = turns[:, :, None] * speeds[None, None, :]
    ends = np.concatenate([flow[:, :, 0], flow[:, :, -1]], axis=1)
    rows = -(-ends.shape[1] // 128)
    ends = np.concatenate([ends, np.repeat(ends[:, :1], rows * 128 - ends.shape[1], axis=1)], axis=1)
    return flow, ends.reshape(2, rows, 128)


def solution(mesh):
    axes = (mesh.shape["gx"], mesh.shape["gy"], mesh.shape["ha"])

    def body(level_set, wind_field):
        nx, ny, nh, nv = level_set.shape
        flow, ends = tables(nv, nh * axes[2])
        n_xy = axes[0] * axes[1]
        state = pltpu.VMEM((nx + 6, nh + 6, ny + 2 * PAD, nv), jnp.float32)
        vmem = pl.BlockSpec(memory_space=pltpu.VMEM)
        increment = pl.pallas_call(
            functools.partial(kernel, (nx, ny, nh, nv), axes),
            out_shape=jax.ShapeDtypeStruct((nx, nh, ny, nv), jnp.float32),
            in_specs=[vmem, pl.BlockSpec(memory_space=pltpu.SMEM), vmem, vmem],
            out_specs=vmem,
            scratch_shapes=[
                state, state, state,
                pltpu.VMEM((nx, nh, ny, nv), jnp.float32),
                pltpu.VMEM((2, nx, ny, nv), jnp.float32),
                pltpu.VMEM((8, 128), jnp.float32),
                pltpu.VMEM((n_xy - 1, 8, 128), jnp.float32),
                pltpu.VMEM((8, nv), jnp.float32),
                pltpu.SemaphoreType.DMA((3, 6)),
                pltpu.SemaphoreType.DMA((3, 6)),
                pltpu.SemaphoreType.DMA((n_xy - 1,)),
                pltpu.SemaphoreType.DMA((n_xy - 1,)),
            ],
            compiler_params=pltpu.CompilerParams(
                collective_id=0, has_side_effects=True, vmem_limit_bytes=56 * 2**20
            ),
        )(level_set.transpose(0, 2, 1, 3), wind_field, jnp.asarray(flow), jnp.asarray(ends))
        return increment.transpose(0, 2, 1, 3)

    return jax.shard_map(
        body,
        mesh=mesh,
        in_specs=(P("gx", "gy", "ha", None), P(None, "gx", "gy")),
        out_specs=P("gx", "gy", "ha", None),
        check_vma=False,
    )
```

time: 162 us -> 83.7 us (0.52)
  Pallas kernels: 0 us -> 81.5 us
  other arithmetic: 65.1 us -> 0 us
  starting transfers between devices: 40.4 us -> 0 us
  waiting for transfers between devices: 22.8 us -> 0 us
  local copies, waits for them, and re-layouts: 19.1 us -> 1.97 us
  blocking collectives: 12.9 us -> 0 us
    pallas_call x0 -> x1, Pallas kernels: none -> 81.5 us  [body(): pl.pallas_call(functools.partial(kernel, (nx, ny, nh, nv), axes), out_sha...]
    add x25 -> x0, other arithmetic: 41.2 us -> none  [the longest x1 17.6 us: body(): level_set + time_step * slope_field(level_set, around_heads(level_set), 0)]
    ppermute x18 -> x0, starting transfers between devices: 40.4 us -> none  [the longest x9 23 us: with_halo(): lax.ppermute(tail, axis, [(i, (i + 1) % count) for i in range(ends)])]
    ppermute x18 -> x0, waiting for transfers between devices: 22.8 us -> none  [the longest x9 14.7 us: with_halo(): lax.ppermute(head, axis, [((i + 1) % count, i) for i in range(ends)])]
    sub x1 -> x0, other arithmetic: 18.4 us -> none  [body(): return advanced - level_set]
    pmax x1 -> x0, blocking collectives: 12.9 us -> none  [body(): top_rate = lax.pmax(local_top, ('gx', 'gy'))]
    slice x29 -> x0, local copies, waits for them, and re-layouts: 12 us -> none  [the longest x9 5.27 us: speed_shifts(): lax.slice_in_dim(values, max(displace, 0), length + min(displace, 0), axi...]
    ppermute x6 -> x0, local copies, waits for them, and re-layouts: 2.79 us -> none  [the longest x3 1.4 us: with_halo(): lax.ppermute(head, axis, [((i + 1) % count, i) for i in range(ends)])]
  transfers between devices with their start and end apart: 18 -> 0, of which waited for: 6 -> 0; matrix products, arithmetic and copies ran while one was open for 13% -> 0% of each run, Pallas kernels for 0% -> 0%
where the time goes in v1:
time: 83.7 us; the launch traced here: 83.5 us
  Pallas kernels  81.5 us (97%)
  local copies, waits for them, and re-layouts  1.97 us (2%)
    pallas_call x1, Pallas kernels, body(): pl.pallas_call(functools.partial(kernel, (nx, ny, nh, nv), axes), out_sha...  81.5 us
    unnamed x1, local copies, waits for them, and re-layouts  1.97 us

profile of v1, /device:TPU:0, one launch (start us, length us, event | category | flops | bytes accessed | tf_op | source)
XLA Modules:
  0.0 83.5 jit_solution(3860482766467561232)
XLA Ops:
  0.0 81.5 %shard_map.46 = f32[8,10,16,128]{3,2,1,0:T(8,128)} custom-call(f32[8,10,16,128]{3,2,1,0:T(8,128)} %bitcast.3, f32[2,8,16]{2,1,0:T(8,128)} %wind_ref.1, f32[2,40,128]{2,1,0:T(8,128)} %constant.4.clone.flow_ref, f32[2,1,128]{2,1,0:T(1,128)} %constant.5.clone.rate_ref), custom_call_target="tpu_custom_call" | custom-call | tf_op jit(solution)/shard_map/pallas_call | solution.py:376
  81.6 2.0 %copy.6 = f32[8,16,10,128]{3,1,2,0:T(8,128)} copy(f32[8,16,10,128]{3,1,2,0:T(8,128)} %bitcast.2) | data formatting | bytes 1310720

commit v2 on v1

--- a/solution.py
+++ b/solution.py
@@ -81,7 +81,7 @@
 
 
 def kernel(sizes, axes, u_ref, wind_ref, flow_ref, rate_ref, out_ref,
-           b0, b1, b2, acc, wind, best, peers, step, sends, recvs, rsend, rrecv):
+           b0, b1, b2, acc, shifted, rights, wind, best, peers, step, sends, recvs, rsend, rrecv):
     nx, ny, nh, nv = sizes
     ngx, ngy, nha = axes
     bufs = (b0, b1, b2)
@@ -172,22 +172,46 @@
             copy, _, has_in = plans[s][i]
             under(has_in, copy.wait_recv)
 
+    def v_shift(buf):
+        def body(i, carry):
+            for j in range(2):
+                for k in range(nh):
+                    u = buf[3 + 2 * i + j, 3 + k, PAD:PAD + ny, :]
+                    for at, move in enumerate((3, 2, 1, nv - 1, nv - 2)):
+                        shifted[at, 2 * i + j, k] = pltpu.roll(u, move, 1)
+            return carry
+
+        lax.fori_loop(0, nx // 2, body, 0)
+
     def v_pass(buf):
         eps = eps_of(d_speed)
         coef = ACCEL_MAX / (3.0 * d_speed)
         e4 = np.float32(np.float32(eps * eps) ** 2)
-        edge = lax.broadcasted_iota(jnp.int32, (ny, nv), 1) == 0
-
-        def one(u):
-            up = lambda a: pltpu.roll(a, 1, 1)
-            down = lambda a: pltpu.roll(a, nv - 1, 1)
-            q = u - up(u)
-            q = jnp.where(edge, down(q), q)
-            qm = up(q)
-            d = jnp.where(edge, 0.0, q - qm)
-            d3 = down(d)
-            e2, f1, s2, f3 = triple(d, d3, eps)
-            e1, e3, s1, s3 = up(e2), down(e2), up(f1), down(f3)
+        lane = lax.broadcasted_iota(jnp.int32, (8, nv), 1)
+        edge = lane == 0
+        keep1 = jnp.where((lane == 1) | (lane == 2), 0.0, 1.0)
+        keep2 = jnp.where(lane < 2, 0.0, 1.0)
+        keep3 = jnp.where((lane == 0) | (lane == nv - 1), 0.0, 1.0)
+        keep4 = jnp.where(lane >= nv - 2, 0.0, 1.0)
+        inner_lane = jnp.where(edge, 0.0, 1.0)
+
+        def one(x, k, t):
+            rows = slice(8 * t, 8 * t + 8)
+            u0 = buf[3 + x, 3 + k, PAD + 8 * t:PAD + 8 * t + 8, :]
+            um3, um2, um1, up1, up2 = [shifted[at, x, k, rows, :] for at in range(5)]
+            qa, qb, qc, qd, qe = um2 - um3, um1 - um2, u0 - um1, up1 - u0, up2 - up1
+            d1 = (qb - qa) * keep1
+            d2 = (qc - qb) * keep2
+            d3 = (qd - qc) * keep3
+            d4 = (qe - qd) * keep4
+            e1 = d2 - d1
+            e2 = d3 - d2
+            e3 = d4 - d3
+            g2 = 0.75 * d2
+            g3 = 0.75 * d3
+            s1 = e1 * e1 + (g2 * (d2 + e1) + eps)
+            s2 = e2 * e2 + (g2 * d3 + eps)
+            s3 = e3 * e3 + (g3 * (d3 - e3) + eps)
             t1 = s2 * s3
             t2 = s1 * s3
             t3 = s1 * s2
@@ -200,19 +224,20 @@
             r3l = jnp.where(edge, e4, r3)
             r2r = jnp.where(edge, r3, r2)
             r1r = jnp.where(edge, e4, r1)
-            al = r1 * jnp.where(edge, 0.0, f12)
-            bl = r3l * f23
-            ar = r1r * f12
-            br = r3 * jnp.where(edge, 0.0, f23)
-            cr = jnp.where(edge, qm, q)
-            left = (3.0 * q + (d3 + 0.5 * d)) + (al + 1.5 * bl) * rcp(r1 + 6.0 * r2l + 3.0 * r3l)
-            right = ((d + 0.5 * d3) - 3.0 * cr) + (1.5 * ar + br) * rcp(3.0 * r1r + 6.0 * r2r + r3)
-            return coef * jnp.minimum(left, down(right))
+            cl = jnp.where(edge, qd, qc)
+            cr = jnp.where(edge, qb, qc)
+            nl = r1 * (f12 * inner_lane) + 1.5 * (r3l * f23)
+            nr = 1.5 * (r1r * f12) + r3 * (f23 * inner_lane)
+            left = (3.0 * cl + (d3 + 0.5 * d2)) + nl * rcp(r1 + 6.0 * r2l + 3.0 * r3l)
+            right = ((d2 + 0.5 * d3) - 3.0 * cr) + nr * rcp(3.0 * r1r + 6.0 * r2r + r3)
+            acc[x, k, rows, :] = coef * left
+            rights[x, k, rows, :] = coef * right
 
         def body(x, carry):
             def inner(k, carry):
                 for j in range(2):
-                    acc[x, 2 * k + j] = one(buf[3 + x, 3 + 2 * k + j, PAD:PAD + ny, :])
+                    for t in range(tiles):
+                        one(x, 2 * k + j, t)
                 return carry
             return lax.fori_loop(0, nh // 2, inner, carry)
 
@@ -248,17 +273,27 @@
     def y_pass(buf):
         eps = eps_of(CELL_SIZE)
 
+        group = math.gcd(nh, 5)
+
+        def one(x, k, row, t):
+            u = [buf[3 + x, 3 + k, PAD + 8 * t + j:PAD + 8 * t + j + 8, :] for j in range(-3, 4)]
+            q = [u[j + 1] - u[j] for j in range(6)]
+            d = [q[j + 1] - q[j] for j in range(5)]
+            fh = (row + wind[1, x, 8 * t:8 * t + 8, :]) * (1.0 / CELL_SIZE)
+            return upwind(*d, q[2], q[3], fh, eps)
+
         def body(x, carry):
-            def inner(k, carry):
-                row = flow_row(1, k)
-                for t in range(tiles):
-                    u = [buf[3 + x, 3 + k, PAD + 8 * t + j:PAD + 8 * t + j + 8, :] for j in range(-3, 4)]
-                    q = [u[j + 1] - u[j] for j in range(6)]
-                    d = [q[j + 1] - q[j] for j in range(5)]
-                    fh = (row + wind[1, x, 8 * t:8 * t + 8, :]) * (1.0 / CELL_SIZE)
-                    acc[x, k, 8 * t:8 * t + 8, :] += upwind(*d, q[2], q[3], fh, eps)
+            def inner(g, carry):
+                speed = [pltpu.roll(rights[x, group * g + j], nv - 1, 1) for j in range(group)]
+                for j in range(group):
+                    k = group * g + j
+                    row = flow_row(1, k)
+                    for t in range(tiles):
+                        rows = slice(8 * t, 8 * t + 8)
+                        along_v = jnp.minimum(acc[x, k, rows, :], speed[j][rows])
+                        acc[x, k, rows, :] = along_v + one(x, k, row, t)
                 return carry
-            return lax.fori_loop(0, nh, inner, carry)
+            return lax.fori_loop(0, nh // group, inner, carry)
 
         lax.fori_loop(0, nx, body, 0)
 
@@ -312,12 +347,11 @@
 
             def act():
                 def body(x, carry):
-                    def inner(k, carry):
+                    for k in range(nh):
                         edge = buf[3 + x, 3 + k, at:at + 1, :]
                         slope = edge - buf[3 + x, 3 + k, near:near + 1, :]
                         buf[3 + x, 3 + k, to:to + 8, :] = edge + reach * slope
-                        return carry
-                    return lax.fori_loop(0, nh, inner, carry)
+                    return carry
                 lax.fori_loop(0, nx, body, 0)
             return act
         pl.when(gy == 0)(ends(True))
@@ -328,6 +362,7 @@
         if s == 0:
             for copy in rate_copies:
                 copy.start()
+        v_shift(bufs[s])
         v_pass(bufs[s])
         fill_y(bufs[s])
         fill_x(bufs[s])
@@ -381,6 +416,8 @@
             scratch_shapes=[
                 state, state, state,
                 pltpu.VMEM((nx, nh, ny, nv), jnp.float32),
+                pltpu.VMEM((5, nx, nh, ny, nv), jnp.float32),
+                pltpu.VMEM((nx, nh, ny, nv), jnp.float32),
                 pltpu.VMEM((2, nx, ny, nv), jnp.float32),
                 pltpu.VMEM((8, 128), jnp.float32),
                 pltpu.VMEM((n_xy - 1, 8, 128), jnp.float32),

time: 83.7 us -> 53.4 us (0.64)
  Pallas kernels: 81.5 us -> 51.3 us
    pallas_call x1, Pallas kernels: 81.5 us -> 51.3 us  [body(): pl.pallas_call(functools.partial(kernel, (nx, ny, nh, nv), axes), out_sha...]
where the time goes in v2:
time: 53.4 us; the launch traced here: 53.3 us
  Pallas kernels  51.3 us (96%)
  local copies, waits for them, and re-layouts  1.97 us (4%)
    pallas_call x1, Pallas kernels, body(): pl.pallas_call(functools.partial(kernel, (nx, ny, nh, nv), axes), out_sha...  51.3 us
    unnamed x1, local copies, waits for them, and re-layouts  1.97 us

profile of v2, /device:TPU:0, one launch (start us, length us, event | category | flops | bytes accessed | tf_op | source)
XLA Modules:
  0.0 53.3 jit_solution(14702178996925001093)
XLA Ops:
  0.0 51.3 %shard_map.46 = f32[8,10,16,128]{3,2,1,0:T(8,128)} custom-call(f32[8,10,16,128]{3,2,1,0:T(8,128)} %bitcast.3, f32[2,8,16]{2,1,0:T(8,128)} %wind_ref.1, f32[2,40,128]{2,1,0:T(8,128)} %constant.4.clone.flow_ref, f32[2,1,128]{2,1,0:T(1,128)} %constant.5.clone.rate_ref), custom_call_target="tpu_custom_call" | custom-call | tf_op jit(solution)/shard_map/pallas_call | solution.py:411
  51.3 2.0 %copy.6 = f32[8,16,10,128]{3,1,2,0:T(8,128)} copy(f32[8,16,10,128]{3,1,2,0:T(8,128)} %bitcast.2) | data formatting | bytes 1310720

commit v3 on v2

--- a/solution.py
+++ b/solution.py
@@ -128,13 +128,12 @@
 
     xs, hs, ys = pl.ds(3, nx), pl.ds(3, nh), pl.ds(PAD, ny)
 
+    parts = math.gcd(nh, 5)
+    part = nh // parts
+
     def copies(s):
         buf = bufs[s]
         plans = (
-            (buf.at[pl.ds(nx, 3), hs, ys], buf.at[pl.ds(0, 3), hs, ys], {"gx": gx + 1},
-             gx < ngx - 1, gx > 0),
-            (buf.at[pl.ds(3, 3), hs, ys], buf.at[pl.ds(3 + nx, 3), hs, ys], {"gx": gx - 1},
-             gx > 0, gx < ngx - 1),
             (buf.at[xs, pl.ds(nh, 3), ys], buf.at[xs, pl.ds(0, 3), ys], up_ha, None, None),
             (buf.at[xs, pl.ds(3, 3), ys], buf.at[xs, pl.ds(3 + nh, 3), ys], down_ha, None, None),
             (buf.at[xs, hs, pl.ds(ny, PAD)], buf.at[xs, hs, pl.ds(0, PAD)], {"gy": gy + 1},
@@ -142,6 +141,14 @@
             (buf.at[xs, hs, pl.ds(PAD, PAD)], buf.at[xs, hs, pl.ds(PAD + ny, PAD)], {"gy": gy - 1},
              gy > 0, gy < ngy - 1),
         )
+        for c in range(parts):
+            hc = pl.ds(3 + c * part, part)
+            plans += (
+                (buf.at[pl.ds(nx, 3), hc, ys], buf.at[pl.ds(0, 3), hc, ys], {"gx": gx + 1},
+                 gx < ngx - 1, gx > 0),
+                (buf.at[pl.ds(3, 3), hc, ys], buf.at[pl.ds(3 + nx, 3), hc, ys], {"gx": gx - 1},
+                 gx > 0, gx < ngx - 1),
+            )
         return [
             (pltpu.make_async_remote_copy(
                 src_ref=src, dst_ref=dst, send_sem=sends.at[s, i], recv_sem=recvs.at[s, i],
@@ -163,8 +170,9 @@
     ]
     plans = [copies(s) for s in range(3)]
 
-    def send_all(s):
-        for copy, has_out, _ in plans[s]:
+    def send(s, which):
+        for i in which:
+            copy, has_out, _ = plans[s][i]
             under(has_out, copy.start)
 
     def wait_in(s, which):
@@ -301,8 +309,8 @@
         buf = bufs[s]
         eps = eps_of(CELL_SIZE)
 
-        def body(i, carry):
-            k = i // tiles
+        def body(first, i, carry):
+            k = first + i // tiles
             base = pl.multiple_of(lax.rem(i, tiles) * 8, 8)
             rows, rows_acc = pl.ds(base + PAD, 8), pl.ds(base, 8)
             row = flow_row(0, k)
@@ -322,7 +330,14 @@
                     out_ref[x, k, rows_acc, :] = (moved - b0[3 + x, 3 + k, rows, :]) * (2.0 / (3.0 * SCALE))
             return carry
 
-        lax.fori_loop(0, nh * tiles, body, 0)
+        for c in range(parts):
+            mine = (4 + 2 * c, 5 + 2 * c)
+            wait_in(s, mine)
+            lax.fori_loop(0, part * tiles, functools.partial(body, c * part), 0)
+            if s < 2:
+                send(s + 1, mine)
+        if s < 2:
+            send(s + 1, range(4))
 
     def fill_x(buf):
         def ends(low):
@@ -358,17 +373,17 @@
         pl.when(gy == ngy - 1)(ends(False))
 
     for s in range(3):
-        send_all(s)
         if s == 0:
+            send(0, range(4 + 2 * parts))
             for copy in rate_copies:
                 copy.start()
         v_shift(bufs[s])
         v_pass(bufs[s])
         fill_y(bufs[s])
         fill_x(bufs[s])
-        wait_in(s, (4, 5))
+        wait_in(s, (2, 3))
         y_pass(bufs[s])
-        wait_in(s, (2, 3))
+        wait_in(s, (0, 1))
         h_pass(bufs[s])
         if s == 0:
             for copy in rate_copies:
@@ -378,7 +393,6 @@
                 top = jnp.maximum(top, peers[delta - 1])
             rate = jnp.max(top, axis=(0, 1), keepdims=True) + (TURN_MAX / d_theta + ACCEL_MAX / d_speed)
             step[...] = jnp.broadcast_to(CFL_NUMBER / rate, step.shape)
-        wait_in(s, (0, 1))
         x_pass(s)
 
     for copy in rate_copies:
@@ -422,8 +436,8 @@
                 pltpu.VMEM((8, 128), jnp.float32),
                 pltpu.VMEM((n_xy - 1, 8, 128), jnp.float32),
                 pltpu.VMEM((8, nv), jnp.float32),
-                pltpu.SemaphoreType.DMA((3, 6)),
-                pltpu.SemaphoreType.DMA((3, 6)),
+                pltpu.SemaphoreType.DMA((3, 4 + 2 * math.gcd(nh, 5))),
+                pltpu.SemaphoreType.DMA((3, 4 + 2 * math.gcd(nh, 5))),
                 pltpu.SemaphoreType.DMA((n_xy - 1,)),
                 pltpu.SemaphoreType.DMA((n_xy - 1,)),
             ],

time: 53.4 us -> 51.5 us (0.964)
  Pallas kernels: 51.3 us -> 49.4 us
    pallas_call x1, Pallas kernels: 51.3 us -> 49.4 us  [body(): pl.pallas_call(functools.partial(kernel, (nx, ny, nh, nv), axes), out_sha...]
where the time goes in v3:
time: 51.5 us; the launch traced here: 51.4 us
  Pallas kernels  49.4 us (96%)
  local copies, waits for them, and re-layouts  1.97 us (4%)
    pallas_call x1, Pallas kernels, body(): pl.pallas_call(functools.partial(kernel, (nx, ny, nh, nv), axes), out_sha...  49.4 us
    unnamed x1, local copies, waits for them, and re-layouts  1.97 us

profile of v3, /device:TPU:0, one launch (start us, length us, event | category | flops | bytes accessed | tf_op | source)
XLA Modules:
  0.0 51.4 jit_solution(9297858308816940)
XLA Ops:
  0.0 49.4 %shard_map.46 = f32[8,10,16,128]{3,2,1,0:T(8,128)} custom-call(f32[8,10,16,128]{3,2,1,0:T(8,128)} %bitcast.3, f32[2,8,16]{2,1,0:T(8,128)} %wind_ref.1, f32[2,40,128]{2,1,0:T(8,128)} %constant.4.clone.flow_ref, f32[2,1,128]{2,1,0:T(1,128)} %constant.5.clone.rate_ref), custom_call_target="tpu_custom_call" | custom-call | tf_op jit(solution)/shard_map/pallas_call | solution.py:425
  49.4 2.0 %copy.6 = f32[8,16,10,128]{3,1,2,0:T(8,128)} copy(f32[8,16,10,128]{3,1,2,0:T(8,128)} %bitcast.2) | data formatting | bytes 1310720
